TPU v7x, 256 devices: a whole 4x4x8 slice. The times are simulated.
256 devices in a mesh: kvp: 32 (over z, x), head: 8 (over y, core).
Axes of the slice: x: 4, y: 4, z: 8, core: 2. Of those that a mesh axis runs over, the one named last changes fastest.
Arguments:
- hidden_in: bfloat16 [16, 8192], P(None, 'kvp'), may hold values from -4 to 4
- attn_gain: bfloat16 [8192], P('kvp'), may hold values from 0.25 to 1.75
- query_key_value_weight: bfloat16 [8192, 8, 1280], P('kvp', 'head'), may hold values from -0.0625 to 0.0625
- k_cache: bfloat16 [8, 2048, 128, 128], P('head', 'kvp'), may hold values from -1200 to 1200
- value_cache: bfloat16 [8, 2048, 128, 128], P('head', 'kvp'), may hold values from -48 to 48
- page_table: int32 [16, 128], P(None, 'kvp'), may hold values from 0 to 63, as said below
- lengths: int32 [16], replicated, may hold values from 4096 to 16384, as said below
- output_weight: bfloat16 [8, 1024, 8192], P('head', None, 'kvp'), may hold values from -0.1875 to 0.1875
- mlp_gain: bfloat16 [8192], P('kvp'), may hold values from 0.099609375 to 1.8984375
- w_in: bfloat16 [8192, 2, 22016], P('kvp', None, 'head'), may hold values from -0.0625 to 0.0625
- w_down: bfloat16 [22016, 8192], P('head', 'kvp'), may hold values from -0.15625 to 0.15625
Outputs:
- next_hidden: bfloat16 [16, 8192], P(None, 'kvp')
Inputs may be any that keep to these rules, and one draw needn't show every extreme that they name: `page_table`: within each aligned block of 4 columns, the 16 x 4 entries are a permutation of 0 to 63. `lengths`: in every draw some request has exactly 16384 cached tokens.
All inputs are finite; a program needn't handle non-finite values.
Results may differ from a plain program's by a relative error of at most 0.033.
Values may be sent and summed in bfloat16 or wider, within the bound.
A program may use at most 64 MiB of HBM per device.

v0:
```python
import jax
import jax.numpy as jnp
from jax import lax
from jax.sharding import Mesh
from jax.sharding import PartitionSpec as P

MODEL_WIDTH = 8192
KVP = ("kvp_0", "kvp_1")


EPSILON = 1e-05
ROPE_BASE = 10000.0


def from_everyone(array, axis):
    copies = jnp.broadcast_to(array, (lax.axis_size(axis), *array.shape))
    return lax.all_to_all(copies, axis, split_axis=0, concat_axis=0, tiled=True)


def of_everyone(array, axis):
    return from_everyone(array, axis).sum(axis=0)


def together(arrays, axis):
    ends = [0]
    for a in arrays:
        ends.append(ends[-1] + a.size)
    total = of_everyone(jnp.concatenate([a.ravel() for a in arrays]), axis)
    return tuple((total[b:e].reshape(a.shape) for a, b, e in zip(arrays, ends, ends[1:])))


def collected_together(array, axis):
    leaves = jax.tree.leaves(array)
    turns = sorted(range(len(leaves)), key=lambda k: -leaves[k].size)
    width = (1, *leaves[turns[0]].shape)[-1]
    lines = [
        jnp.pad(leaves[k].reshape(-1), (0, -leaves[k].size % width)).reshape(-1, width)
        for k in turns
    ]
    both, at, found = (lax.all_gather(jnp.concatenate(lines), axis), 0, {})
    for k, line in zip(turns, lines):
        section = both[:, at : at + len(line)].reshape(len(both), -1)
        found[k] = section[:, : leaves[k].size].reshape(-1, *leaves[k].shape)
        at += len(line)
    numbers = iter(range(len(leaves)))
    return jax.tree.map(lambda _: found[next(numbers)], array)


def combined_by_axis(array, axes, combine):
    for axis in axes:
        pieces = collected_together(array, axis)
        array = jax.tree.map(lambda part: part[0], pieces)
        for k in range(1, lax.axis_size(axis)):
            array = combine(array, jax.tree.map(lambda part: part[k], pieces))
    return array


def in_blocks(array, dim, size):
    before, after = (array.shape[:dim], array.shape[dim + 1 :])
    return jnp.moveaxis(array.reshape(*before, size, -1, *after), dim, 0)


def summed_on_arrival(array, axis, dim):
    size = lax.axis_size(axis)
    tiles = lax.all_to_all(in_blocks(array, dim, size), axis, 0, 0, tiled=True)
    return jnp.sum(tiles.astype(jnp.float32), axis=0)


def in_order(tiles, dim):
    lengths = list(tiles.shape[1:])
    lengths[dim] *= tiles.shape[0]
    return jnp.moveaxis(tiles, 0, dim).reshape(lengths)


def gather_directly(array, axis, dim):
    return in_order(from_everyone(array, axis), dim)


def rotate(vector, position):
    half_size = vector.shape[-1] // 2
    exponent = jnp.arange(half_size, dtype=jnp.float32) * (2.0 / vector.shape[-1])
    inverse = ROPE_BASE ** (-exponent)
    angles = position.astype(jnp.float32)[:, None] * inverse[None, :]
    target_shape = (angles.shape[0],) + (1,) * (vector.ndim - 2) + (half_size,)
    cosine = jnp.cos(angles).reshape(target_shape)
    sine_part = jnp.sin(angles).reshape(target_shape)
    front_half = vector[..., :half_size]
    back_half = vector[..., half_size:]
    return jnp.concatenate(
        [front_half * cosine - back_half * sine_part, back_half * cosine + front_half * sine_part],
        axis=-1,
    )


def join_parts(former, latter):
    maxima = jnp.maximum(former[0], latter[0])
    weight_former = jnp.exp(former[0] - maxima)
    weight_latter = jnp.exp(latter[0] - maxima)
    totals = former[1] * weight_former + latter[1] * weight_latter
    summed = former[2] * weight_former[..., None] + latter[2] * weight_latter[..., None]
    return (maxima, totals, summed)


def on_device(
    hidden_in,
    attn_gain,
    query_key_value_weight,
    k_cache,
    value_cache,
    page_table,
    lengths,
    output_weight,
    mlp_gain,
    w_in,
    w_down,
):
    requests = hidden_in.shape[0]
    heads_here = query_key_value_weight.shape[1]
    page_size = k_cache.shape[2]
    head_size = k_cache.shape[3]
    groups = output_weight.shape[1] // head_size
    stream = hidden_in.astype(jnp.float32)
    normed = (stream * attn_gain.astype(jnp.float32)).astype(jnp.bfloat16)
    partial_value = jnp.dot(
        normed,
        query_key_value_weight.reshape(query_key_value_weight.shape[0], -1),
        preferred_element_type=jnp.float32,
    )
    squares = jnp.sum(stream * stream, axis=1)
    projected_rows, square_sum = together((partial_value, squares), KVP)
    attention_scale = lax.rsqrt(square_sum / MODEL_WIDTH + EPSILON)
    projected_rows = (projected_rows * attention_scale[:, None]).reshape(
        requests, heads_here, groups + 2, head_size
    )
    queries = rotate(projected_rows[:, :, :groups, :], lengths).astype(jnp.bfloat16)
    new_keys = rotate(projected_rows[:, :, groups, :], lengths).astype(jnp.bfloat16)
    new_values = projected_rows[:, :, groups + 1, :].astype(jnp.bfloat16)
    pages_here = page_table.shape[1]
    shard_index = lax.axis_index(KVP)
    page_start = (shard_index * pages_here + jnp.arange(pages_here, dtype=jnp.int32)) * page_size
    positions = (page_start[:, None] + jnp.arange(page_size, dtype=jnp.int32)[None, :]).reshape(-1)
    live_mask = positions[None, :] < lengths[:, None]
    slot_rows = page_table.reshape(-1)
    factor = head_size ** (-0.5)
    cached_keys = k_cache[0][slot_rows].reshape(requests, -1, head_size)
    cached_values = value_cache[0][slot_rows].reshape(requests, -1, head_size)
    scores = (
        jnp.einsum("bgd,bld->bgl", queries[:, 0], cached_keys, preferred_element_type=jnp.float32)
        * factor
    )
    scores = jnp.where(live_mask[:, None, :], scores, -1e30)
    local_max = jnp.max(scores, axis=-1)
    weights = jnp.where(live_mask[:, None, :], jnp.exp(scores - local_max[..., None]), 0.0)
    max_list = [local_max]
    total_list = [jnp.sum(weights, axis=-1)]
    summed_list = [
        jnp.einsum(
            "bgl,bld->bgd",
            weights.astype(jnp.bfloat16),
            cached_values,
            preferred_element_type=jnp.float32,
        )
    ]
    maxima = jnp.stack(max_list, axis=1)
    totals = jnp.stack(total_list, axis=1)
    summed = jnp.stack(summed_list, axis=1)
    maxima, totals, summed = combined_by_axis((maxima, totals, summed), KVP, join_parts)
    query_float = queries.astype(jnp.float32)
    own = jnp.sum(query_float * new_keys.astype(jnp.float32)[:, :, None, :], axis=-1) * factor
    overall = jnp.maximum(maxima, own)
    carried = jnp.exp(maxima - overall)
    own_weight = jnp.exp(own - overall)
    totals = totals * carried + own_weight
    own_rounded = lax.optimization_barrier(own_weight.astype(jnp.bfloat16)).astype(jnp.float32)
    summed = (
        summed * carried[..., None]
        + own_rounded[..., None] * new_values.astype(jnp.float32)[:, :, None, :]
    )
    attn = (summed / totals[..., None]).astype(jnp.bfloat16).reshape(requests, -1)
    out_term = jnp.dot(
        attn, output_weight.reshape(-1, output_weight.shape[2]), preferred_element_type=jnp.float32
    )
    stream = stream + of_everyone(out_term, "head")
    normed_mlp = (stream * mlp_gain.astype(jnp.float32)).astype(jnp.bfloat16)
    both_parts = jnp.dot(
        normed_mlp, w_in.reshape(w_in.shape[0], -1), preferred_element_type=jnp.float32
    )
    both_parts = both_parts.reshape(requests, 2, w_in.shape[2])
    squares_mlp = jnp.sum(stream * stream, axis=1)
    shares = summed_on_arrival(both_parts.astype(jnp.bfloat16), KVP, 2)
    square_mlp_sum = of_everyone(squares_mlp, KVP)
    scale_mlp = lax.rsqrt(square_mlp_sum / MODEL_WIDTH + EPSILON)
    gate_part = shares[:, 0] * scale_mlp[:, None]
    up_part = shares[:, 1] * scale_mlp[:, None]
    hidden_share = (jax.nn.silu(gate_part) * up_part).astype(jnp.bfloat16)
    down_term = jnp.dot(
        gather_directly(hidden_share, KVP, 1), w_down, preferred_element_type=jnp.float32
    )
    result = stream + of_everyone(down_term, "head")
    return result.astype(jnp.bfloat16)


def solution(mesh):
    split = Mesh(mesh.devices.reshape(8, 4, mesh.shape["head"]), ("kvp_0", "kvp_1", "head"))
    return jax.shard_map(
        on_device,
        mesh=split,
        in_specs=(
            P(None, KVP),
            P(KVP),
            P(KVP, "head", None),
            P("head", KVP, None, None),
            P("head", KVP, None, None),
            P(None, KVP),
            P(),
            P("head", None, KVP),
            P(KVP),
            P(KVP, None, "head"),
            P("head", KVP),
        ),
        out_specs=P(None, KVP),
        check_vma=False,
    )
```

profile of v0, /device:TPU:1, one launch (start us, length us, event | category | flops | bytes accessed | tf_op | source)
XLA Modules:
  0.0 198.3 jit_solution(9742608192641907591)
XLA Ops:
  0.0 0.8 convert_element_type.108
  0.8 0.9 fusion.52
  1.7 1.3 fusion.2
  3.0 2.9 %broadcast_in_dim.29 = f32[32,1,20496]{2,1,0:T(1,128)} broadcast(f32[20496]{0:T(1024)S(1)} %pad_maximum_fusion), dimensions={2} | broadcast | bytes 2705472 | tf_op jit(solution)/shard_map/broadcast_in_dim | solution.py:16
  5.9 12.1 %all-to-all-start = ((f32[32,1,20496]{2,1,0:T(1,128)}), f32[32,1,20496]{2,1,0:T(1,128)}, u32[]{:S(2)}, u32[]{:S(2)}) async-start(f32[32,1,20496]{2,1,0:T(1,128)} %broadcast_in_dim.29), calls=%async_computation | async-start | bytes 5275648 | tf_op jit(solution)/shard_map/all_to_all | solution.py:17
  18.1 0.1 reshape.1836
  18.3 3.8 %gather_fusion = bf16[64,128,128]{2,1,0:T(8,128)(2,1)} fusion(bf16[64,128,128]{2,1,0:T(8,128)(2,1)} %bitcast.431, s32[1024]{0:T(1024)S(1)} %pad_clamp_fusion), kind=kCustom, calls=%fused_computation | custom fusion | bytes 4194560 | tf_op jit(solution)/shard_map/gather | solution.py:145
  22.0 3.8 %gather_fusion.1 = bf16[64,128,128]{2,1,0:T(8,128)(2,1)} fusion(bf16[64,128,128]{2,1,0:T(8,128)(2,1)} %bitcast.432, s32[1024]{0:T(1024)S(1)} %pad_clamp_fusion), kind=kCustom, calls=%fused_computation.1 | custom fusion | bytes 4194560 | tf_op jit(solution)/shard_map/gather | solution.py:146
  26.0 0.1 multiply_cosine_fusion.1
  26.1 52.0 %all-to-all-done = f32[32,1,20496]{2,1,0:T(1,128)} async-done(((f32[32,1,20496]{2,1,0:T(1,128)}), f32[32,1,20496]{2,1,0:T(1,128)}, u32[]{:S(2)}, u32[]{:S(2)}) %all-to-all-start) | async-done | bytes 2623520 | tf_op jit(solution)/shard_map/all_to_all | solution.py:17
  78.1 3.2 %reduce_sum.82 = f32[20496]{0:T(1024)S(1)} reduce(f32[32,1,20496]{2,1,0:T(1,128)} %all-to-all-done, f32[]{:T(128)} %constant.10.clone.1), dimensions={0,1}, to_apply=%region_1.0 | reduce | flops 635376 | bytes 2705476 | tf_op jit(solution)/shard_map/reduce_sum | solution.py:21
  81.5 0.1 subtract_convert_fusion
  81.6 2.4 %fusion.121 = (f32[16,8]{1,0:T(8,128)S(1)}, f32[16,8,512]{2,1,0:T(8,128)S(1)}) fusion(bf16[16,512,128]{2,1,0:T(8,128)(2,1)} %bitcast.430, bf16[16,8,64]{2,1,0:T(8,128)(2,1)S(1)} %bitcast.435, bf16[16,8,64]{2,1,0:T(8,128)(2,1)S(1)} %bitcast.434, pred[16,512]{1,0:T(8,128)(4,1)S(1)} %broadcast_compare_fusion), kind=kOutput, calls=%fused_computation.231 | convolution fusion | flops 17039232 | bytes 2400768 | tf_op jit(solution)/shard_map/bgd,bld->bgl/dot_general | solution.py:148
  83.9 0.1 reshape.1840
  84.0 0.2 fusion.6
  84.2 2.0 %convolution_bitcast_fusion = f32[128,128]{1,0:T(8,128)S(1)} fusion(bf16[16,512,128]{2,1,0:T(8,128)(2,1)} %bitcast.429, f32[16,8,512]{2,1,0:T(8,128)S(1)} %get-tuple-element.54, f32[16,8]{1,0:T(8,128)S(1)} %get-tuple-element.53, pred[16,512]{1,0:T(8,128)(4,1)S(1)} %broadcast_compare_fusion), kind=kOutput, calls=%fused_computation.6 | convolution fusion | flops 16973824 | bytes 2433536 | tf_op jit(solution)/shard_map/bgl,bld->bgd/dot_general | solution.py:157
  86.3 0.1 reshape.1841
  86.4 19.6 %all-gather.2 = f32[8,130,128]{2,1,0:T(8,128)S(1)} all-gather(f32[1,130,128]{2,1,0:T(8,128)S(1)} %maximum_bitcast_fusion), channel_id=2, replica_groups=mesh['kvp_0'=8,'kvp_1'=4,'head'=8] {'kvp_0'}, dimensions={0}, use_global_device_ids=true | all-gather | bytes 599040 | tf_op jit(solution)/shard_map/all_gather | solution.py:40
  106.1 0.3 fusion.25
  106.4 11.3 %all-gather.3 = f32[4,130,128]{2,1,0:T(8,128)S(1)} all-gather(f32[1,130,128]{2,1,0:T(8,128)S(1)} %maximum_bitcast_fusion.1), channel_id=3, replica_groups=mesh['kvp_0'=8,'kvp_1'=4,'head'=8] {'kvp_1'}, dimensions={0}, use_global_device_ids=true | all-gather | bytes 332800 | tf_op jit(solution)/shard_map/all_gather | solution.py:40
  118.0 0.1 squeeze.179
  118.1 0.1 squeeze.181
  118.2 0.1 squeeze.184
  118.3 0.1 squeeze.185
  118.3 0.1 squeeze.186
  118.4 0.1 squeeze.187
  118.5 0.1 fusion.77
  118.8 0.2 multiply_reduce_fusion
  119.3 0.2 fusion.45
  119.5 1.2 fusion.4
  120.8 0.7 broadcast_in_dim.32
  121.4 14.1 %all-to-all-start.1 = ((f32[8,16,256]{2,1,0:T(8,128)}), f32[8,16,256]{2,1,0:T(8,128)S(1)}, u32[]{:S(2)}, u32[]{:S(2)}) async-start(f32[8,16,256]{2,1,0:T(8,128)} %broadcast_in_dim.32), calls=%async_computation.1 | async-start | bytes 262144 | tf_op jit(solution)/shard_map/all_to_all | solution.py:17
  135.5 5.2 %all-to-all-done.1 = f32[8,16,256]{2,1,0:T(8,128)S(1)} async-done(((f32[8,16,256]{2,1,0:T(8,128)}), f32[8,16,256]{2,1,0:T(8,128)S(1)}, u32[]{:S(2)}, u32[]{:S(2)}) %all-to-all-start.1) | async-done | bytes 131104 | tf_op jit(solution)/shard_map/all_to_all | solution.py:17
  140.8 0.1 multiply_reduce_fusion.1
  140.9 0.6 broadcast_in_dim.33
  141.5 5.9 %all-to-all-start.3 = ((f32[32,1,16]{2,1,0:T(1,128)}), f32[32,1,16]{2,1,0:T(1,128)S(1)}, u32[]{:S(2)}, u32[]{:S(2)}) async-start(f32[32,1,16]{2,1,0:T(1,128)} %broadcast_in_dim.33), calls=%async_computation.3 | async-start | bytes 32768 | tf_op jit(solution)/shard_map/all_to_all | solution.py:17
  147.5 0.8 convolution_convert_fusion
  148.3 0.9 reshape.1844
  149.2 0.8 copy.51
  150.0 6.0 %all-to-all-done.3 = f32[32,1,16]{2,1,0:T(1,128)S(1)} async-done(((f32[32,1,16]{2,1,0:T(1,128)}), f32[32,1,16]{2,1,0:T(1,128)S(1)}, u32[]{:S(2)}, u32[]{:S(2)}) %all-to-all-start.3) | async-done | bytes 2080 | tf_op jit(solution)/shard_map/all_to_all | solution.py:17
  156.1 3.9 %all-to-all-start.2 = ((bf16[32,16,2,86]{3,1,2,0:T(8,128)(2,1)}), bf16[32,16,2,86]{3,1,2,0:T(8,128)(2,1)S(1)}, u32[]{:S(2)}, u32[]{:S(2)}) async-start(bf16[32,16,2,86]{3,1,2,0:T(8,128)(2,1)} %bitcast.428), calls=%async_computation.2 | async-start | bytes 524288 | tf_op jit(solution)/shard_map/all_to_all | solution.py:65
  160.0 10.5 %all-to-all-done.2 = bf16[32,16,2,86]{3,1,2,0:T(8,128)(2,1)S(1)} async-done(((bf16[32,16,2,86]{3,1,2,0:T(8,128)(2,1)}), bf16[32,16,2,86]{3,1,2,0:T(8,128)(2,1)S(1)}, u32[]{:S(2)}, u32[]{:S(2)}) %all-to-all-start.2) | async-done | bytes 176160 | tf_op jit(solution)/shard_map/all_to_all | solution.py:65
  170.6 0.1 fusion.69
  170.7 13.4 %all_to_all.32 = bf16[32,16,86]{2,1,0:T(8,128)(2,1)S(1)} all-to-all(bf16[32,16,86]{2,1,0:T(8,128)(2,1)S(1)} %broadcast_in_dim.34), channel_id=1, replica_groups=mesh['kvp_0'=8,'kvp_1'=4,'head'=8] {'kvp_0','kvp_1'}, dimensions={0} | all-to-all | bytes 176128 | tf_op jit(solution)/shard_map/all_to_all | solution.py:17
  184.1 0.2 reshape.1845
  184.3 1.6 fusion.122
  186.0 11.7 %all_to_all.33 = f32[8,16,256]{2,1,0:T(8,128)S(1)} all-to-all(f32[8,16,256]{2,1,0:T(8,128)S(1)} %broadcast_in_dim.35), channel_id=1, replica_groups=mesh['kvp_0'=8,'kvp_1'=4,'head'=8] {'head'}, dimensions={0} | all-to-all | bytes 262144 | tf_op jit(solution)/shard_map/all_to_all | solution.py:17
  197.7 0.6 add_convert_fusion.1
  (54 shorter events, 1.4 us)
Async XLA Ops:
  0.0 147.5 %copy-start = (bf16[256,2,2752]{0,2,1:T(8,128)(2,1)S(1)}, bf16[256,2,2752]{0,2,1:T(8,128)(2,1)}, u32[]{:S(2)}) copy-start(bf16[256,2,2752]{0,2,1:T(8,128)(2,1)} %param.20) | copy-start | bytes 8454148
  5.9 12.1 %copy-start.3 = (s32[16]{0:T(128)S(1)}, s32[16]{0:T(128)}, u32[]{:S(2)}) copy-start(s32[16]{0:T(128)} %param.17) | copy-start | bytes 196
  5.9 12.1 %copy-start.2 = (s32[16,4]{0,1:T(4,128)S(1)}, s32[16,4]{0,1:T(4,128)}, u32[]{:S(2)}) copy-start(s32[16,4]{0,1:T(4,128)} %param.16) | copy-start | bytes 772
  5.9 72.2 %all-to-all-start = ((f32[32,1,20496]{2,1,0:T(1,128)}), f32[32,1,20496]{2,1,0:T(1,128)}, u32[]{:S(2)}, u32[]{:S(2)}) async-start(f32[32,1,20496]{2,1,0:T(1,128)} %broadcast_in_dim.29), calls=%async_computation | async-start | bytes 5275648 | tf_op jit(solution)/shard_map/all_to_all | solution.py:17
  86.3 49.3 %copy-start.4 = (bf16[256]{0:T(256)(128)(2,1)S(1)}, bf16[256]{0:T(256)(128)(2,1)}, u32[]{:S(2)}) copy-start(bf16[256]{0:T(256)(128)(2,1)} %param.19) | copy-start | bytes 1540
  86.3 54.5 %copy-start.1 = (bf16[16,256]{1,0:T(8,128)(2,1)S(1)}, bf16[16,256]{1,0:T(8,128)(2,1)}, u32[]{:S(2)}) copy-start(bf16[16,256]{1,0:T(8,128)(2,1)} %param.11) | copy-start | bytes 24580
  121.4 19.4 %all-to-all-start.1 = ((f32[8,16,256]{2,1,0:T(8,128)}), f32[8,16,256]{2,1,0:T(8,128)S(1)}, u32[]{:S(2)}, u32[]{:S(2)}) async-start(f32[8,16,256]{2,1,0:T(8,128)} %broadcast_in_dim.32), calls=%async_computation.1 | async-start | bytes 262144 | tf_op jit(solution)/shard_map/all_to_all | solution.py:17
  141.5 14.6 %all-to-all-start.3 = ((f32[32,1,16]{2,1,0:T(1,128)}), f32[32,1,16]{2,1,0:T(1,128)S(1)}, u32[]{:S(2)}, u32[]{:S(2)}) async-start(f32[32,1,16]{2,1,0:T(1,128)} %broadcast_in_dim.33), calls=%async_computation.3 | async-start | bytes 32768 | tf_op jit(solution)/shard_map/all_to_all | solution.py:17
  156.1 14.5 %all-to-all-start.2 = ((bf16[32,16,2,86]{3,1,2,0:T(8,128)(2,1)}), bf16[32,16,2,86]{3,1,2,0:T(8,128)(2,1)S(1)}, u32[]{:S(2)}, u32[]{:S(2)}) async-start(bf16[32,16,2,86]{3,1,2,0:T(8,128)(2,1)} %bitcast.428), calls=%async_computation.2 | async-start | bytes 524288 | tf_op jit(solution)/shard_map/all_to_all | solution.py:65
where the time goes:
time: 199 us; the launch traced here: 198 us
  waiting for transfers between devices  73.8 us (37%)
  blocking collectives  56 us (28%)
  starting transfers between devices  36 us (18%)
  local copies, waits for them, and re-layouts  15.2 us (8%)
  matrix products  9.37 us (5%)
  other arithmetic  7.66 us (4%)
    all_to_all x3, waiting for transfers between devices, from_everyone(): return lax.all_to_all(copies, axis, split_axis=0, concat_axis=0, tiled=True)  63.2 us
    all_to_all x3, starting transfers between devices, from_everyone(): return lax.all_to_all(copies, axis, split_axis=0, concat_axis=0, tiled=True)  32.1 us
    all_gather x2, blocking collectives, collected_together(): both, at, found = (lax.all_gather(jnp.concatenate(lines), axis), 0, {})  31 us
    all_to_all x2, blocking collectives, from_everyone(): return lax.all_to_all(copies, axis, split_axis=0, concat_axis=0, tiled=True)  25.1 us
    all_to_all x1, waiting for transfers between devices, summed_on_arrival(): tiles = lax.all_to_all(in_blocks(array, dim, size), axis, 0, 0, tiled=True)  10.5 us
    broadcast_in_dim x5, local copies, waits for them, and re-layouts, from_everyone(): copies = jnp.broadcast_to(array, (lax.axis_size(axis), *array.shape))  4.22 us
  transfers between devices with their start and end apart: 4, of which 4 were waited for; matrix products, arithmetic and copies ran while one was open for 5% of the time, Pallas kernels for 0%

commit v1 on v0

v1 whole, which is shorter than its diff:
```python
import functools
import math

import jax
import jax.numpy as jnp
import numpy as np
from jax import lax
from jax.experimental import pallas as pl
from jax.experimental.pallas import tpu as pltpu
from jax.sharding import PartitionSpec as P

MESH = pl.DeviceIdType.MESH
F32 = jnp.float32
BF16 = jnp.bfloat16

MODEL_WIDTH = 8192
EPSILON = 1e-05
ROPE_BASE = 10000.0
B = 16
G = 8
D = 128
N = 32
H = 8
PAGE = 128
PAGES_HERE = 4
TILES_QKV = G + 2
LANES = 128

SPREAD, UNSPREAD = 5, 13


def iota(shape, dim):
    return lax.broadcasted_iota(jnp.int32, shape, dim)


def to_row(column):
    wide = jnp.broadcast_to(column, (B, LANES))
    kept = jnp.where(iota((B, LANES), 0) == iota((B, LANES), 1), wide, 0.0)
    return jnp.sum(kept, axis=0, keepdims=True)


def to_column(row):
    wide = jnp.broadcast_to(row, (B, LANES))
    kept = jnp.where(iota((B, LANES), 0) == iota((B, LANES), 1), wide, 0.0)
    return jnp.sum(kept, axis=1, keepdims=True)


def sine_and_cosine(angle):
    turns = jnp.floor(angle * (1.0 / (2.0 * math.pi)) + 0.5)
    left = angle - turns * 6.28125
    left = left - turns * (2.0 * math.pi - 6.28125)
    y = left * 0.5
    z = y * y
    sine, cosine = 0.0, 0.0
    for k in range(6, -1, -1):
        sine = sine * z + (-1.0) ** k / math.factorial(2 * k + 1)
    for k in range(7, -1, -1):
        cosine = cosine * z + (-1.0) ** k / math.factorial(2 * k)
    sine = sine * y
    return 2.0 * sine * cosine, 1.0 - 2.0 * sine * sine


def kernel(
    tiles_ff,
    ff,
    hidden_hbm,
    attn_gain_ref,
    qkv_hbm,
    k_hbm,
    v_hbm,
    table_ref,
    lengths_ref,
    wo_hbm,
    mlp_gain_ref,
    win_hbm,
    wdown_hbm,
    inverse_ref,
    out_ref,
    hidden,
    wqkv,
    keys,
    values,
    wo,
    win,
    wdown,
    qkv_send,
    qkv_recv,
    square_send,
    square_recv,
    q_all,
    q_rows,
    part_send,
    part_recv,
    attn_all,
    attn_rows,
    head_send,
    head_recv,
    ff_send,
    ff_recv,
    square2_send,
    square2_recv,
    hid_all,
    last_send,
    last_recv,
    local_sem,
    send_sem,
    recv_sem,
):
    me = lax.axis_index("kvp")
    my_head = lax.axis_index("head")
    mine = lax.rem(me * UNSPREAD, N)

    def copy_to(src, dst, phase, device):
        pltpu.make_async_remote_copy(
            src_ref=src,
            dst_ref=dst,
            send_sem=send_sem.at[phase],
            recv_sem=recv_sem.at[phase],
            device_id=device,
            device_id_type=MESH,
        ).start()

    def waiter(ref, phase):
        return pltpu.make_async_remote_copy(
            src_ref=ref,
            dst_ref=ref,
            send_sem=send_sem.at[phase],
            recv_sem=recv_sem.at[phase],
            device_id={"kvp": lax.rem(me + 1, N)},
            device_id_type=MESH,
        )

    def loads():
        yield hidden_hbm, hidden
        yield qkv_hbm, wqkv
        yield k_hbm.at[pl.ds(0, 32)], keys.at[pl.ds(0, 32)]
        yield k_hbm.at[pl.ds(32, 32)], keys.at[pl.ds(32, 32)]
        yield v_hbm.at[pl.ds(0, 32)], values.at[pl.ds(0, 32)]
        yield v_hbm.at[pl.ds(32, 32)], values.at[pl.ds(32, 32)]
        yield wo_hbm, wo
        yield win_hbm.at[0], win.at[0, pl.ds(0, ff)]
        yield win_hbm.at[1], win.at[1, pl.ds(0, ff)]
        yield wdown_hbm, wdown.at[pl.ds(0, ff)]

    copies = [
        pltpu.make_async_copy(src, dst, local_sem.at[at]) for at, (src, dst) in enumerate(loads())
    ]
    for copy in copies:
        copy.start()

    barrier = pltpu.get_barrier_semaphore()

    @pl.loop(1, N)
    def _(step):
        pl.semaphore_signal(
            barrier, inc=1, device_id={"kvp": lax.rem(me + step, N)}, device_id_type=MESH
        )

    @pl.loop(1, H)
    def _(step):
        pl.semaphore_signal(
            barrier, inc=1, device_id={"head": lax.rem(my_head + step, H)}, device_id_type=MESH
        )

    pad = win.shape[1] - ff
    win[:, pl.ds(ff, pad), :] = jnp.zeros((2, pad, win.shape[2]), BF16)
    wdown[pl.ds(ff, pad), :] = jnp.zeros((pad, wdown.shape[1]), BF16)

    rows = iota((B, LANES), 0)
    position = jnp.zeros((B, LANES), F32)
    for b in range(B):
        position = jnp.where(rows == b, lengths_ref[b].astype(F32), position)
    sine, cosine = sine_and_cosine(position * inverse_ref[0:1, :])
    sine = jnp.where(iota((B, LANES), 1) < D // 2, -sine, sine)

    copies[0].wait()
    copies[1].wait()
    x = hidden[...].astype(F32)
    normed = (x * attn_gain_ref[...][None, :].astype(F32)).astype(BF16)
    partial = jnp.dot(normed, wqkv[...], preferred_element_type=F32).astype(BF16)
    for t in range(TILES_QKV):
        qkv_send[t] = partial[:, t * D : (t + 1) * D]
    square_row = to_row(jnp.sum(x * x, axis=1, keepdims=True))
    square_send[...] = square_row

    pl.semaphore_wait(barrier, N - 1 + H - 1)

    def scatter(tiles, send):
        @pl.loop(1, N)
        def _(step):
            t = lax.rem(mine + step, N)

            @pl.when(t < tiles)
            def _():
                send(t, {"kvp": lax.rem(t * SPREAD, N)})

    def spread(all_ref, phase):
        @pl.loop(1, N)
        def _(step):
            copy_to(
                all_ref.at[mine], all_ref.at[mine], phase, {"kvp": lax.rem(me + step, N)}
            )

    def wait_gathered(all_ref, tiles, phase):
        @pl.when(mine < tiles)
        def _():
            waiter(all_ref.at[pl.ds(0, tiles - 1)], phase).wait_recv()

        @pl.when(mine >= tiles)
        def _():
            waiter(all_ref, phase).wait_recv()

    def send_qkv(t, device):
        copy_to(qkv_send.at[t], qkv_recv.at[me], 0, device)
        copy_to(square_send, square_recv.at[me], 1, device)

    scatter(TILES_QKV, send_qkv)

    @pl.when(mine < TILES_QKV)
    def _():
        qkv_recv[me] = qkv_send[mine]
        square_recv[me] = square_row
        waiter(square_recv.at[pl.ds(0, N - 1)], 1).wait_recv()
        waiter(qkv_recv.at[pl.ds(0, N - 1)], 0).wait_recv()
        square = to_column(jnp.sum(square_recv[...], axis=0))
        scale = lax.rsqrt(square / MODEL_WIDTH + EPSILON)
        total = jnp.sum(qkv_recv[...].astype(F32), axis=0) * scale
        turned = total * cosine + pltpu.roll(total, D // 2, 1) * sine
        q_all[mine] = jnp.where(mine < G + 1, turned, total).astype(BF16)
        spread(q_all, 2)

    for copy in copies[2:6]:
        copy.wait()
    wait_gathered(q_all, TILES_QKV, 2)

    q_rows[...] = q_all[...].astype(F32).reshape(TILES_QKV * B, D)
    factor = D ** (-0.5)
    lane = iota((G, LANES), 1)
    first = me * (PAGES_HERE * PAGE)
    for b in range(B):
        query = q_rows[pl.ds(b, G, stride=B), :].astype(BF16)
        left = lengths_ref[b] - first
        slots = [table_ref[p, b] for p in range(PAGES_HERE)]
        scores, live = [], []
        for p in range(PAGES_HERE):
            score = lax.dot_general(
                query, keys[slots[p]], (((1,), (1,)), ((), ())), preferred_element_type=F32
            )
            live.append(lane + p * PAGE < left)
            scores.append(jnp.where(live[p], score * factor, -1e30))
        top = functools.reduce(jnp.maximum, scores)
        top = jnp.max(top, axis=1, keepdims=True)
        weights = [jnp.where(ok, jnp.exp(s - top), 0.0) for ok, s in zip(live, scores)]
        total = jnp.sum(functools.reduce(jnp.add, weights), axis=1, keepdims=True)
        summed = 0.0
        for p in range(PAGES_HERE):
            summed = summed + jnp.dot(
                weights[p].astype(BF16), values[slots[p]], preferred_element_type=F32
            )
        high = top.astype(BF16).astype(F32)
        middle = (top - high).astype(BF16).astype(F32)
        low = top - high - middle
        stats = jnp.where(
            lane < 32, high, jnp.where(lane < 64, middle, jnp.where(lane < 96, low, total))
        )
        part_send[b] = jnp.concatenate([summed, stats], axis=0).astype(BF16)

    def send_part(t, device):
        copy_to(part_send.at[t], part_recv.at[me], 3, device)

    scatter(B, send_part)

    @pl.when(mine < B)
    def _():
        query = q_rows[pl.ds(mine, G, stride=B), :]
        new_key = q_rows[pl.ds(G * B + mine, 1), :]
        new_value = q_rows[pl.ds((G + 1) * B + mine, 1), :]
        own = jnp.sum(query * new_key, axis=1, keepdims=True) * factor
        part_recv[me] = part_send[mine]
        waiter(part_recv.at[pl.ds(0, N - 1)], 3).wait_recv()
        tops, overall = [], own
        for k in range(N):
            stats = part_recv[k].astype(F32)[G:]
            tops.append(stats[:, 0:1] + stats[:, 32:33] + stats[:, 64:65])
            overall = jnp.maximum(overall, tops[k])
        own_weight = jnp.exp(own - overall)
        total = own_weight
        summed = own_weight.astype(BF16).astype(F32) * new_value
        for k in range(N):
            tile = part_recv[k].astype(F32)
            carried = jnp.exp(tops[k] - overall)
            total = total + tile[G:, 96:97] * carried
            summed = summed + tile[:G] * carried
        attn_all[mine] = (summed / total).astype(BF16)
        spread(attn_all, 4)

    copies[6].wait()
    wait_gathered(attn_all, B, 4)

    attn_rows[...] = attn_all[...].astype(F32).reshape(B * G, D)
    attn = jnp.concatenate(
        [attn_rows[pl.ds(g, B, stride=G), :].astype(BF16) for g in range(G)], axis=1
    )

    def over_heads(term, send_ref, recv_ref, phase):
        send_ref[...] = term.astype(BF16)
        recv_ref[my_head] = term.astype(BF16)

        @pl.loop(1, H)
        def _(step):
            copy_to(
                send_ref, recv_ref.at[my_head], phase, {"head": lax.rem(my_head + step, H)}
            )

        waiter(recv_ref.at[pl.ds(0, H - 1)], phase).wait_recv()
        return jnp.sum(recv_ref[...].astype(F32), axis=0)

    term = jnp.dot(attn, wo[...], preferred_element_type=F32)
    stream = x + over_heads(term, head_send, head_recv, 5)

    square2_row = to_row(jnp.sum(stream * stream, axis=1, keepdims=True))
    square2_send[...] = square2_row
    normed = (stream * mlp_gain_ref[...][None, :].astype(F32)).astype(BF16)
    copies[7].wait()
    copies[8].wait()
    for t in range(tiles_ff):
        for part in range(2):
            ff_send[t, part] = lax.dot_general(
                normed,
                win[part, pl.ds(t * LANES, LANES), :],
                (((1,), (1,)), ((), ())),
                preferred_element_type=F32,
            ).astype(BF16)

    def send_ff(t, device):
        copy_to(ff_send.at[t], ff_recv.at[me], 6, device)
        copy_to(square2_send, square2_recv.at[me], 7, device)

    scatter(tiles_ff, send_ff)

    @pl.when(mine < tiles_ff)
    def _():
        ff_recv[me] = ff_send[mine]
        square2_recv[me] = square2_row
        waiter(square2_recv.at[pl.ds(0, N - 1)], 7).wait_recv()
        waiter(ff_recv.at[pl.ds(0, N - 1)], 6).wait_recv()
        square = to_column(jnp.sum(square2_recv[...], axis=0))
        scale = lax.rsqrt(square / MODEL_WIDTH + EPSILON)
        both = jnp.sum(ff_recv[...].astype(F32), axis=0)
        gate, up = both[0] * scale, both[1] * scale
        hid_all[mine] = (gate / (1.0 + jnp.exp(-gate)) * up).astype(BF16)
        spread(hid_all, 8)

    copies[9].wait()
    wait_gathered(hid_all, tiles_ff, 8)

    active = jnp.concatenate([hid_all[t] for t in range(tiles_ff)], axis=1)
    term = jnp.dot(active, wdown[...], preferred_element_type=F32)
    out_ref[...] = (stream + over_heads(term, last_send, last_recv, 9)).astype(BF16)

    def wait_scattered(recv_ref, tiles, phase):
        @pl.when(mine < tiles)
        def _():
            waiter(recv_ref.at[pl.ds(0, tiles - 1)], phase).wait_send()

        @pl.when(mine >= tiles)
        def _():
            waiter(recv_ref.at[pl.ds(0, tiles)], phase).wait_send()

    wait_scattered(qkv_recv, TILES_QKV, 0)
    wait_scattered(square_recv, TILES_QKV, 1)
    wait_scattered(part_recv, B, 3)
    wait_scattered(ff_recv, tiles_ff, 6)
    wait_scattered(square2_recv, tiles_ff, 7)

    @pl.when(mine < TILES_QKV)
    def _():
        waiter(qkv_recv.at[pl.ds(0, N - 1)], 2).wait_send()

    @pl.when(mine < B)
    def _():
        waiter(part_recv.at[pl.ds(0, N - 1), pl.ds(0, G)], 4).wait_send()

    @pl.when(mine < tiles_ff)
    def _():
        waiter(part_recv.at[pl.ds(0, N - 1)], 8).wait_send()

    waiter(head_recv.at[pl.ds(0, H - 1)], 5).wait_send()
    waiter(last_recv.at[pl.ds(0, H - 1)], 9).wait_send()


def on_device(
    hidden_in,
    attn_gain,
    query_key_value_weight,
    k_cache,
    value_cache,
    page_table,
    lengths,
    output_weight,
    mlp_gain,
    w_in,
    w_down,
):
    width = hidden_in.shape[1]
    ff = w_down.shape[0]
    tiles_ff = -(-ff // LANES)
    half = D // 2
    inverse = ROPE_BASE ** (-np.arange(half, dtype=np.float64) * (2.0 / D))
    inverse = np.broadcast_to(np.concatenate([inverse, inverse]), (8, D)).astype(np.float32)
    any_space = pl.BlockSpec(memory_space=pl.ANY)
    vmem = pl.BlockSpec(memory_space=pltpu.VMEM)
    smem = pl.BlockSpec(memory_space=pltpu.SMEM)
    slots = k_cache.shape[1]
    return pl.pallas_call(
        functools.partial(kernel, tiles_ff, ff),
        out_shape=jax.ShapeDtypeStruct((B, width), BF16),
        in_specs=[
            any_space,
            vmem,
            any_space,
            any_space,
            any_space,
            smem,
            smem,
            any_space,
            vmem,
            any_space,
            any_space,
            vmem,
        ],
        out_specs=vmem,
        scratch_shapes=[
            pltpu.VMEM((B, width), BF16),
            pltpu.VMEM((width, TILES_QKV * D), BF16),
            pltpu.VMEM((slots, PAGE, D), BF16),
            pltpu.VMEM((slots, PAGE, D), BF16),
            pltpu.VMEM((G * D, width), BF16),
            pltpu.VMEM((2, tiles_ff * LANES, width), BF16),
            pltpu.VMEM((tiles_ff * LANES, width), BF16),
            pltpu.VMEM((TILES_QKV, B, D), BF16),
            pltpu.VMEM((N, B, D), BF16),
            pltpu.VMEM((1, LANES), F32),
            pltpu.VMEM((N, 1, LANES), F32),
            pltpu.VMEM((TILES_QKV, B, D), BF16),
            pltpu.VMEM((TILES_QKV * B, D), F32),
            pltpu.VMEM((B, 2 * G, D), BF16),
            pltpu.VMEM((N, 2 * G, D), BF16),
            pltpu.VMEM((B, G, D), BF16),
            pltpu.VMEM((B * G, D), F32),
            pltpu.VMEM((B, width), BF16),
            pltpu.VMEM((H, B, width), BF16),
            pltpu.VMEM((tiles_ff, 2, B, LANES), BF16),
            pltpu.VMEM((N, 2, B, LANES), BF16),
            pltpu.VMEM((1, LANES), F32),
            pltpu.VMEM((N, 1, LANES), F32),
            pltpu.VMEM((tiles_ff, B, LANES), BF16),
            pltpu.VMEM((B, width), BF16),
            pltpu.VMEM((H, B, width), BF16),
            pltpu.SemaphoreType.DMA((10,)),
            pltpu.SemaphoreType.DMA((10,)),
            pltpu.SemaphoreType.DMA((10,)),
        ],
        compiler_params=pltpu.CompilerParams(collective_id=0, has_side_effects=True),
    )(
        hidden_in,
        attn_gain,
        query_key_value_weight.transpose(1, 0, 2)[0],
        k_cache[0],
        value_cache[0],
        page_table.T,
        lengths,
        output_weight[0],
        mlp_gain,
        w_in.transpose(1, 2, 0),
        w_down,
        jnp.asarray(inverse),
    )


def solution(mesh):
    return jax.shard_map(
        on_device,
        mesh=mesh,
        in_specs=(
            P(None, "kvp"),
            P("kvp"),
            P("kvp", "head", None),
            P("head", "kvp", None, None),
            P("head", "kvp", None, None),
            P(None, "kvp"),
            P(),
            P("head", None, "kvp"),
            P("kvp"),
            P("kvp", None, "head"),
            P("head", "kvp"),
        ),
        out_specs=P(None, "kvp"),
        check_vma=False,
    )
```

time: 199 us -> 67.4 us (0.34)
  waiting for transfers between devices: 73.8 us -> 0 us
  Pallas kernels: 0 us -> 65.8 us
  blocking collectives: 56 us -> 0 us
  starting transfers between devices: 36 us -> 0 us
  local copies, waits for them, and re-layouts: 15.2 us -> 1.3 us
  matrix products: 9.37 us -> 0 us
  other arithmetic: 7.66 us -> 0 us
    all_to_all x4 -> x0, waiting for transfers between devices: 73.8 us -> none  [the longest x3 63.2 us: from_everyone(): return lax.all_to_all(copies, axis, split_axis=0, concat_axis=0, tiled=True)]
    pallas_call x0 -> x1, Pallas kernels: none -> 65.8 us  [on_device(): pl.pallas_call(functools.partial(kernel, tiles_ff, ff), out_shape=jax.Sha...]
    all_to_all x4 -> x0, starting transfers between devices: 36 us -> none  [the longest x3 32.1 us: from_everyone(): return lax.all_to_all(copies, axis, split_axis=0, concat_axis=0, tiled=True)]
    all_gather x2 -> x0, blocking collectives: 31 us -> none  [collected_together(): both, at, found = (lax.all_gather(jnp.concatenate(lines), axis), 0, {})]
    all_to_all x2 -> x0, blocking collectives: 25.1 us -> none  [from_everyone(): return lax.all_to_all(copies, axis, split_axis=0, concat_axis=0, tiled=True)]
    dot_general x6 -> x0, matrix products: 9.37 us -> none  [the longest x1 2.35 us: on_device(): jnp.einsum('bgd,bld->bgl', queries[:, 0], cached_keys, preferred_element_...]
    gather x2 -> x0, local copies, waits for them, and re-layouts: 7.56 us -> none  [the longest x1 3.78 us: on_device(): cached_values = value_cache[0][slot_rows].reshape(requests, -1, head_size)]
    reduce_sum x9 -> x0, other arithmetic: 4.73 us -> none  [the longest x4 3.32 us: of_everyone(): return from_everyone(array, axis).sum(axis=0)]
  transfers between devices with their start and end apart: 4 -> 0, of which waited for: 4 -> 0; matrix products, arithmetic and copies ran while one was open for 5% -> 0% of each run, Pallas kernels for 0% -> 0%
where the time goes in v1:
time: 67.4 us; the launch traced here: 67.1 us
  Pallas kernels  65.8 us (98%)
  local copies, waits for them, and re-layouts  1.3 us (2%)
    pallas_call x1, Pallas kernels, on_device(): pl.pallas_call(functools.partial(kernel, tiles_ff, ff), out_shape=jax.Sha...  65.8 us

profile of v1, /device:TPU:1, one launch (start us, length us, event | category | flops | bytes accessed | tf_op | source)
XLA Modules:
  0.0 67.1 jit_solution(11426779409575897189)
XLA Ops:
  0.0 65.8 %shard_map.118 = bf16[16,256]{1,0:T(8,128)(2,1)} custom-call(bf16[16,256]{1,0:T(8,128)(2,1)} %hidden_hbm.1, bf16[256]{0:T(256)(128)(2,1)} %attn_gain_ref.1, bf16[256,1280]{1,0:T(8,128)(2,1)} %bitcast.9, bf16[64,128,128]{2,1,0:T(8,128)(2,1)} %bitcast.7, bf16[64,128,128]{2,1,0:T(8,128)(2,1)} %bitcast.8, s32[4,16]{1,0:T(4,128)} %bitcast.11, s32[16]{0:T(128)} %lengths_ref.1, ...), custom_call_target="tpu_custom_call" | custom-call | tf_op jit(solution)/shard_map/pallas_call | solution.py:415
  65.8 1.3 %copy.14 = bf16[16,256]{1,0:T(8,128)(2,1)} copy(bf16[16,256]{1,0:T(8,128)(2,1)} %shard_map.118) | data formatting | bytes 16384

commit v2 on v1

v2 whole, which is shorter than its diff:
```python
import functools
import math

import jax
import jax.numpy as jnp
import numpy as np
from jax import lax
from jax.experimental import pallas as pl
from jax.experimental.pallas import tpu as pltpu
from jax.sharding import PartitionSpec as P

MESH = pl.DeviceIdType.MESH
F32 = jnp.float32
BF16 = jnp.bfloat16

MODEL_WIDTH = 8192
EPSILON = 1e-05
ROPE_BASE = 10000.0
B = 16
G = 8
D = 128
Z, X = 8, 4
N = Z * X
Y, C = 4, 2
H = Y * C
PAGE = 128
PAGES_HERE = 4
VECTORS = G + 2
LANES = 128
SQUARE_ROW = VECTORS
GROUP = 8


def around(offset, size):
    return min(offset % size, -offset % size)


def far_first(offsets, sizes):
    return sorted(offsets, key=lambda at: -sum(around(o, s) for o, s in zip(at, sizes)))


ALL = far_first([(dz, dx) for dz in range(Z) for dx in range(X) if (dz, dx) != (0, 0)], (Z, X))
NEAR = far_first(
    [(dz, dx) for dz in (-1, 0, 1, 2) for dx in range(X) if (dz, dx) != (0, 0)], (Z, X)
)
HEADS = far_first([(dy, dc) for dy in range(Y) for dc in range(C) if (dy, dc) != (0, 0)], (Y, C))


def iota(shape, dim):
    return lax.broadcasted_iota(jnp.int32, shape, dim)


def to_row(column):
    wide = jnp.broadcast_to(column, (B, LANES))
    kept = jnp.where(iota((B, LANES), 0) == iota((B, LANES), 1), wide, 0.0)
    return jnp.sum(kept, axis=0, keepdims=True)


def to_column(row):
    wide = jnp.broadcast_to(row, (B, LANES))
    kept = jnp.where(iota((B, LANES), 0) == iota((B, LANES), 1), wide, 0.0)
    return jnp.sum(kept, axis=1, keepdims=True)


def rounded(value):
    return value.astype(BF16).astype(F32)


def sine_and_cosine(angle):
    turns = jnp.floor(angle * (1.0 / (2.0 * math.pi)) + 0.5)
    left = angle - turns * 6.28125
    left = left - turns * (2.0 * math.pi - 6.28125)
    y = left * 0.5
    z = y * y
    sine, cosine = 0.0, 0.0
    for k in range(6, -1, -1):
        sine = sine * z + (-1.0) ** k / math.factorial(2 * k + 1)
    sine = sine * y
    for k in range(7, -1, -1):
        cosine = cosine * z + (-1.0) ** k / math.factorial(2 * k)
    return 2.0 * sine * cosine, 1.0 - 2.0 * sine * sine


def kernel(
    tiles_ff,
    ff,
    hidden_hbm,
    attn_gain_hbm,
    qkv_hbm,
    k_hbm,
    v_hbm,
    table_hbm,
    lengths_hbm,
    wo_hbm,
    mlp_gain_hbm,
    win_hbm,
    wdown_hbm,
    inverse_hbm,
    out_ref,
    hidden,
    attn_gain,
    mlp_gain,
    inverse,
    table,
    lengths,
    wqkv,
    keys,
    values,
    wo,
    win,
    wdown,
    turned,
    qkv_send,
    qkv_recv,
    q_all,
    part_send,
    part_recv,
    attn_all,
    attn_rows,
    head_send,
    head_recv,
    ff_send,
    ff_recv,
    square_send,
    square_recv,
    hid_all,
    last_send,
    last_recv,
    local_sem,
    send_sem,
    recv_sem,
):
    me = lax.axis_index("kvp")
    my_head = lax.axis_index("head")
    my_z, my_x = me // X, lax.rem(me, X)
    my_y, my_c = my_head // C, lax.rem(my_head, C)
    zs = [lax.rem(my_z + dz, Z) for dz in range(Z)]
    xs = [lax.rem(my_x + dx, X) for dx in range(X)]
    ys = [lax.rem(my_y + dy, Y) for dy in range(Y)]
    cs = [lax.rem(my_c + dc, C) for dc in range(C)]

    def peer(dz, dx):
        return {"kvp": zs[dz % Z] * X + xs[dx % X]}

    def head_peer(dy, dc):
        return {"head": ys[dy] * C + cs[dc]}

    request_of_z = [lax.rem(z, Z // 2) * X for z in zs]
    tile_of_z = [lax.rem(z * 20, N) for z in zs]
    tile_of_x = [x * 13 for x in xs]

    def request_at(dz, dx):
        return request_of_z[dz % Z] + xs[dx % X]

    def tile_at(dz, dx):
        return lax.rem(tile_of_z[dz % Z] + tile_of_x[dx % X], N)

    my_request = request_at(0, 0)
    my_tile = tile_at(0, 0)

    def copy_to(src, dst, phase, device):
        pltpu.make_async_remote_copy(
            src_ref=src,
            dst_ref=dst,
            send_sem=send_sem.at[phase],
            recv_sem=recv_sem.at[phase],
            device_id=device,
            device_id_type=MESH,
        ).start()

    def waiter(ref, phase):
        return pltpu.make_async_remote_copy(
            src_ref=ref,
            dst_ref=ref,
            send_sem=send_sem.at[phase],
            recv_sem=recv_sem.at[phase],
            device_id=peer(1, 0),
            device_id_type=MESH,
        )

    barrier = pltpu.get_barrier_semaphore()
    for offset in ALL:
        pl.semaphore_signal(barrier, inc=1, device_id=peer(*offset), device_id_type=MESH)
    for offset in HEADS:
        pl.semaphore_signal(barrier, inc=1, device_id=head_peer(*offset), device_id_type=MESH)

    pairs = [
        (hidden_hbm, hidden),
        (attn_gain_hbm, attn_gain),
        (qkv_hbm, wqkv),
        (lengths_hbm, lengths),
        (inverse_hbm, inverse),
        (table_hbm, table),
        (k_hbm.at[pl.ds(0, 32)], keys.at[pl.ds(0, 32)]),
        (k_hbm.at[pl.ds(32, 32)], keys.at[pl.ds(32, 32)]),
        (v_hbm.at[pl.ds(0, 32)], values.at[pl.ds(0, 32)]),
        (v_hbm.at[pl.ds(32, 32)], values.at[pl.ds(32, 32)]),
        (wo_hbm, wo),
        (mlp_gain_hbm, mlp_gain),
        (win_hbm.at[0], win.at[0, pl.ds(0, ff)]),
        (win_hbm.at[1], win.at[1, pl.ds(0, ff)]),
        (wdown_hbm, wdown.at[pl.ds(0, ff)]),
    ]
    copies = [
        pltpu.make_async_copy(src, dst, local_sem.at[at]) for at, (src, dst) in enumerate(pairs)
    ]
    for copy in copies:
        copy.start()

    pad = win.shape[1] - ff
    win[:, pl.ds(ff, pad), :] = jnp.zeros((2, pad, win.shape[2]), BF16)
    wdown[pl.ds(ff, pad), :] = jnp.zeros((pad, wdown.shape[1]), BF16)
    turned[...] = jnp.zeros(turned.shape, F32)

    for copy in copies[:3]:
        copy.wait()
    x = hidden[...].astype(F32)
    normed = (x * attn_gain[...][None, :].astype(F32)).astype(BF16)
    partial = jnp.dot(normed, wqkv[...], preferred_element_type=F32)
    for v in range(VECTORS):
        turned[pl.ds(v, B, stride=2 * G), :] = partial[:, v * D : (v + 1) * D]
    square = jnp.sum(x * x, axis=1, keepdims=True)
    high = rounded(square)
    turned[pl.ds(SQUARE_ROW, B, stride=2 * G), :] = jnp.where(
        iota((B, LANES), 1) < LANES // 2, high, square - high
    )
    qkv_send[...] = turned[...].reshape(B, 2 * G, D).astype(BF16)
    qkv_recv[me] = qkv_send[my_request]

    pl.semaphore_wait(barrier, len(ALL) + len(HEADS))

    for offset in ALL:
        copy_to(qkv_send.at[request_at(*offset)], qkv_recv.at[me], 0, peer(*offset))
    for copy in copies[3:6]:
        copy.wait()
    sine, cosine = sine_and_cosine(lengths[my_request].astype(F32) * inverse[...])
    lane = iota((G, LANES), 1)
    sine = jnp.where(lane < D // 2, -sine, sine)[0:1]
    cosine = cosine[0:1]
    for copy in copies[6:10]:
        copy.wait()
    waiter(qkv_recv.at[pl.ds(0, len(ALL))], 0).wait_recv()
    total = jnp.sum(qkv_recv[...].astype(F32), axis=0)
    square = total[SQUARE_ROW : SQUARE_ROW + 1]
    square = square[:, 0:1] + square[:, LANES // 2 : LANES // 2 + 1]
    total = total * lax.rsqrt(square / MODEL_WIDTH + EPSILON)
    rotated = total * cosine + pltpu.roll(total, D // 2, 1) * sine
    q_all[my_request] = rotated[:G].astype(BF16)
    for offset in NEAR:
        copy_to(q_all.at[my_request], q_all.at[my_request], 1, peer(*offset))
    factor = D ** (-0.5)
    new_key, new_value = rounded(rotated[G : G + 1]), rounded(total[G + 1 : G + 2])
    own = jnp.sum(rounded(rotated[:G]) * new_key, axis=1, keepdims=True) * factor
    waiter(q_all.at[pl.ds(0, len(NEAR))], 1).wait_recv()

    first = me * (PAGES_HERE * PAGE)
    slots = [[table[p, b] for p in range(PAGES_HERE)] for b in range(B)]
    scores = [
        [
            lax.dot_general(
                q_all[b], keys[slot], (((1,), (1,)), ((), ())), preferred_element_type=F32
            )
            for slot in slots[b]
        ]
        for b in range(B)
    ]
    parts = []
    for b in range(B):
        left = lengths[b] - first
        live = [lane + p * PAGE < left for p in range(PAGES_HERE)]
        masked = [jnp.where(ok, s * factor, -1e30) for ok, s in zip(live, scores[b])]
        top = jnp.max(functools.reduce(jnp.maximum, masked), axis=1, keepdims=True)
        weights = [jnp.where(ok, jnp.exp(s - top), 0.0) for ok, s in zip(live, masked)]
        total = jnp.sum(functools.reduce(jnp.add, weights), axis=1, keepdims=True)
        summed = 0.0
        for p in range(PAGES_HERE):
            summed = summed + jnp.dot(
                weights[p].astype(BF16), values[slots[b][p]], preferred_element_type=F32
            )
        high = rounded(top)
        middle = rounded(top - high)
        low = top - high - middle
        stats = jnp.where(
            lane < 32, high, jnp.where(lane < 64, middle, jnp.where(lane < 96, low, total))
        )
        parts.append(jnp.concatenate([summed, stats], axis=0).astype(BF16))
    for b in range(B):
        part_send[b] = parts[b]

    for offset in ALL:
        copy_to(part_send.at[request_at(*offset)], part_recv.at[me], 2, peer(*offset))
    part_recv[me] = part_send[my_request]
    copies[10].wait()
    waiter(part_recv.at[pl.ds(0, len(ALL))], 2).wait_recv()
    tops, overall = [], own
    for k in range(N):
        stats = part_recv[k].astype(F32)[G:]
        tops.append(stats[:, 0:1] + stats[:, 32:33] + stats[:, 64:65])
        overall = jnp.maximum(overall, tops[k])
    own_weight = jnp.exp(own - overall)
    total = own_weight
    summed = rounded(own_weight) * new_value
    for k in range(N):
        tile = part_recv[k].astype(F32)
        carried = jnp.exp(tops[k] - overall)
        total = total + tile[G:, 96:97] * carried
        summed = summed + tile[:G] * carried
    attn_all[my_request] = (summed / total).astype(BF16)
    for offset in NEAR:
        copy_to(attn_all.at[my_request], attn_all.at[my_request], 3, peer(*offset))
    waiter(attn_all.at[pl.ds(0, len(NEAR))], 3).wait_recv()

    attn_rows[...] = attn_all[...].astype(F32).reshape(B * G, D)
    attn = jnp.concatenate(
        [attn_rows[pl.ds(g, B, stride=G), :].astype(BF16) for g in range(G)], axis=1
    )

    def over_heads(term, send_ref, recv_ref, phase):
        send_ref[...] = term.astype(BF16)
        for offset in HEADS:
            copy_to(send_ref, recv_ref.at[my_head], phase, head_peer(*offset))
        recv_ref[my_head] = term.astype(BF16)
        waiter(recv_ref.at[pl.ds(0, len(HEADS))], phase).wait_recv()
        return jnp.sum(recv_ref[...].astype(F32), axis=0)

    term = jnp.dot(attn, wo[...], preferred_element_type=F32)
    for copy in copies[11:14]:
        copy.wait()
    stream = x + over_heads(term, head_send, head_recv, 4)

    square_row = to_row(jnp.sum(stream * stream, axis=1, keepdims=True))
    square_send[...] = square_row
    normed = (stream * mlp_gain[...][None, :].astype(F32)).astype(BF16)
    for start in range(0, N, GROUP):
        group = (ALL + [(0, 0)])[start : start + GROUP]
        for offset in group:
            tile = tile_at(*offset)
            rows = pl.ds(pl.multiple_of(jnp.minimum(tile, tiles_ff - 1) * LANES, LANES), LANES)
            for part in range(2):
                ff_send[tile, part] = lax.dot_general(
                    normed,
                    win[part, rows, :],
                    (((1,), (1,)), ((), ())),
                    preferred_element_type=F32,
                ).astype(BF16)
        for offset in group:
            if offset != (0, 0):
                tile = tile_at(*offset)

                @pl.when(tile < tiles_ff)
                def _(tile=tile, offset=offset):
                    copy_to(ff_send.at[tile], ff_recv.at[me], 5, peer(*offset))
                    copy_to(square_send, square_recv.at[me], 6, peer(*offset))

    @pl.when(my_tile < tiles_ff)
    def _():
        ff_recv[me] = ff_send[my_tile]
        square_recv[me] = square_row
        waiter(square_recv.at[pl.ds(0, N - 1)], 6).wait_recv()
        waiter(ff_recv.at[pl.ds(0, N - 1)], 5).wait_recv()
        square = to_column(jnp.sum(square_recv[...], axis=0))
        scale = lax.rsqrt(square / MODEL_WIDTH + EPSILON)
        both = jnp.sum(ff_recv[...].astype(F32), axis=0)
        gate, up = both[0] * scale, both[1] * scale
        hid_all[my_tile] = (gate / (1.0 + jnp.exp(-gate)) * up).astype(BF16)
        for offset in ALL:
            copy_to(hid_all.at[my_tile], hid_all.at[my_tile], 7, peer(*offset))
        waiter(hid_all.at[pl.ds(0, tiles_ff - 1)], 7).wait_recv()

    @pl.when(my_tile >= tiles_ff)
    def _():
        waiter(hid_all, 7).wait_recv()

    copies[14].wait()
    active = jnp.concatenate([hid_all[t] for t in range(tiles_ff)], axis=1)
    term = jnp.dot(active, wdown[...], preferred_element_type=F32)
    out_ref[...] = (stream + over_heads(term, last_send, last_recv, 8)).astype(BF16)

    waiter(qkv_recv.at[pl.ds(0, len(ALL))], 0).wait_send()
    waiter(q_all.at[pl.ds(0, len(NEAR))], 1).wait_send()
    waiter(part_recv.at[pl.ds(0, len(ALL))], 2).wait_send()
    waiter(attn_all.at[pl.ds(0, len(NEAR))], 3).wait_send()
    waiter(head_recv.at[pl.ds(0, len(HEADS))], 4).wait_send()
    waiter(last_recv.at[pl.ds(0, len(HEADS))], 8).wait_send()

    @pl.when(my_tile < tiles_ff)
    def _():
        waiter(ff_recv.at[pl.ds(0, tiles_ff - 1)], 5).wait_send()
        waiter(square_recv.at[pl.ds(0, tiles_ff - 1)], 6).wait_send()
        waiter(part_recv.at[pl.ds(0, N - 1)], 7).wait_send()

    @pl.when(my_tile >= tiles_ff)
    def _():
        waiter(ff_recv.at[pl.ds(0, tiles_ff)], 5).wait_send()
        waiter(square_recv.at[pl.ds(0, tiles_ff)], 6).wait_send()


def on_device(
    hidden_in,
    attn_gain,
    query_key_value_weight,
    k_cache,
    value_cache,
    page_table,
    lengths,
    output_weight,
    mlp_gain,
    w_in,
    w_down,
):
    width = hidden_in.shape[1]
    ff = w_down.shape[0]
    tiles_ff = -(-ff // LANES)
    half = D // 2
    inverse = ROPE_BASE ** (-np.arange(half, dtype=np.float64) * (2.0 / D))
    inverse = np.broadcast_to(np.concatenate([inverse, inverse]), (8, D)).astype(np.float32)
    slots = k_cache.shape[1]
    return pl.pallas_call(
        functools.partial(kernel, tiles_ff, ff),
        out_shape=jax.ShapeDtypeStruct((B, width), BF16),
        in_specs=[pl.BlockSpec(memory_space=pl.ANY)] * 12,
        out_specs=pl.BlockSpec(memory_space=pltpu.VMEM),
        scratch_shapes=[
            pltpu.VMEM((B, width), BF16),
            pltpu.VMEM((width,), BF16),
            pltpu.VMEM((width,), BF16),
            pltpu.VMEM((8, D), F32),
            pltpu.SMEM((PAGES_HERE, B), jnp.int32),
            pltpu.SMEM((B,), jnp.int32),
            pltpu.VMEM((width, VECTORS * D), BF16),
            pltpu.VMEM((slots, PAGE, D), BF16),
            pltpu.VMEM((slots, PAGE, D), BF16),
            pltpu.VMEM((G * D, width), BF16),
            pltpu.VMEM((2, tiles_ff * LANES, width), BF16),
            pltpu.VMEM((tiles_ff * LANES, width), BF16),
            pltpu.VMEM((B * 2 * G, D), F32),
            pltpu.VMEM((B, 2 * G, D), BF16),
            pltpu.VMEM((N, 2 * G, D), BF16),
            pltpu.VMEM((B, G, D), BF16),
            pltpu.VMEM((B, 2 * G, D), BF16),
            pltpu.VMEM((N, 2 * G, D), BF16),
            pltpu.VMEM((B, G, D), BF16),
            pltpu.VMEM((B * G, D), F32),
            pltpu.VMEM((B, width), BF16),
            pltpu.VMEM((H, B, width), BF16),
            pltpu.VMEM((N, 2, B, LANES), BF16),
            pltpu.VMEM((N, 2, B, LANES), BF16),
            pltpu.VMEM((1, LANES), F32),
            pltpu.VMEM((N, 1, LANES), F32),
            pltpu.VMEM((tiles_ff, B, LANES), BF16),
            pltpu.VMEM((B, width), BF16),
            pltpu.VMEM((H, B, width), BF16),
            pltpu.SemaphoreType.DMA((15,)),
            pltpu.SemaphoreType.DMA((9,)),
            pltpu.SemaphoreType.DMA((9,)),
        ],
        compiler_params=pltpu.CompilerParams(collective_id=0, has_side_effects=True),
    )(
        hidden_in,
        attn_gain,
        query_key_value_weight.transpose(1, 0, 2)[0],
        k_cache[0],
        value_cache[0],
        page_table.T,
        lengths,
        output_weight[0],
        mlp_gain,
        w_in.transpose(1, 2, 0),
        w_down,
        jnp.asarray(inverse),
    )


def solution(mesh):
    return jax.shard_map(
        on_device,
        mesh=mesh,
        in_specs=(
            P(None, "kvp"),
            P("kvp"),
            P("kvp", "head", None),
            P("head", "kvp", None, None),
            P("head", "kvp", None, None),
            P(None, "kvp"),
            P(),
            P("head", None, "kvp"),
            P("kvp"),
            P("kvp", None, "head"),
            P("head", "kvp"),
        ),
        out_specs=P(None, "kvp"),
        check_vma=False,
    )
```

time: 67.4 us -> 58.4 us (0.87)
  Pallas kernels: 65.8 us -> 56.9 us
    pallas_call x1, Pallas kernels: 65.8 us -> 56.9 us  [on_device(): pl.pallas_call(functools.partial(kernel, tiles_ff, ff), out_shape=jax.Sha...]
where the time goes in v2:
time: 58.4 us; the launch traced here: 58.2 us
  Pallas kernels  56.9 us (97%)
  local copies, waits for them, and re-layouts  1.3 us (2%)
    pallas_call x1, Pallas kernels, on_device(): pl.pallas_call(functools.partial(kernel, tiles_ff, ff), out_shape=jax.Sha...  56.9 us
    unnamed x1, local copies, waits for them, and re-layouts  1.3 us

profile of v2, /device:TPU:1, one launch (start us, length us, event | category | flops | bytes accessed | tf_op | source)
XLA Modules:
  0.0 58.2 jit_solution(3307305803357402053)
XLA Ops:
  0.0 56.9 %shard_map.118 = bf16[16,256]{1,0:T(8,128)(2,1)} custom-call(bf16[16,256]{1,0:T(8,128)(2,1)} %hidden_hbm.1, bf16[256]{0:T(256)(128)(2,1)} %attn_gain_hbm.1, bf16[256,1280]{1,0:T(8,128)(2,1)} %bitcast.9, bf16[64,128,128]{2,1,0:T(8,128)(2,1)} %bitcast.7, bf16[64,128,128]{2,1,0:T(8,128)(2,1)} %bitcast.8, s32[4,16]{1,0:T(4,128)} %bitcast.11, s32[16]{0:T(128)} %lengths_hbm.1, ...), custom_call_target="tpu_custom_call" | custom-call | tf_op jit(solution)/shard_map/pallas_call | solution.py:418
  56.9 1.3 %copy.14 = bf16[16,256]{1,0:T(8,128)(2,1)} copy(bf16[16,256]{1,0:T(8,128)(2,1)} %shard_map.118) | data formatting | bytes 16384

commit v3 on v2

--- a/solution.py
+++ b/solution.py
@@ -28,7 +28,9 @@
 VECTORS = G + 2
 LANES = 128
 SQUARE_ROW = VECTORS
-GROUP = 8
+GROUP = 7
+OWNERS = 16
+SPREAD, UNSPREAD = 5, 13
 
 
 def around(offset, size):
@@ -113,6 +115,7 @@
     qkv_send,
     qkv_recv,
     q_all,
+    pair,
     part_send,
     part_recv,
     attn_all,
@@ -146,17 +149,12 @@
         return {"head": ys[dy] * C + cs[dc]}
 
     request_of_z = [lax.rem(z, Z // 2) * X for z in zs]
-    tile_of_z = [lax.rem(z * 20, N) for z in zs]
-    tile_of_x = [x * 13 for x in xs]
 
     def request_at(dz, dx):
         return request_of_z[dz % Z] + xs[dx % X]
 
-    def tile_at(dz, dx):
-        return lax.rem(tile_of_z[dz % Z] + tile_of_x[dx % X], N)
-
     my_request = request_at(0, 0)
-    my_tile = tile_at(0, 0)
+    my_tile = lax.rem(me * UNSPREAD, N)
 
     def copy_to(src, dst, phase, device):
         pltpu.make_async_remote_copy(
@@ -177,12 +175,6 @@
             device_id=peer(1, 0),
             device_id_type=MESH,
         )
-
-    barrier = pltpu.get_barrier_semaphore()
-    for offset in ALL:
-        pl.semaphore_signal(barrier, inc=1, device_id=peer(*offset), device_id_type=MESH)
-    for offset in HEADS:
-        pl.semaphore_signal(barrier, inc=1, device_id=head_peer(*offset), device_id_type=MESH)
 
     pairs = [
         (hidden_hbm, hidden),
@@ -204,7 +196,18 @@
     copies = [
         pltpu.make_async_copy(src, dst, local_sem.at[at]) for at, (src, dst) in enumerate(pairs)
     ]
-    for copy in copies:
+    for copy in copies[:3]:
+        copy.start()
+    barrier = pltpu.get_barrier_semaphore()
+
+    @pl.when(me < OWNERS)
+    def _():
+        for offset in ALL:
+            pl.semaphore_signal(barrier, inc=1, device_id=peer(*offset), device_id_type=MESH)
+
+    for offset in HEADS:
+        pl.semaphore_signal(barrier, inc=1, device_id=head_peer(*offset), device_id_type=MESH)
+    for copy in copies[3:]:
         copy.start()
 
     pad = win.shape[1] - ff
@@ -225,12 +228,19 @@
         iota((B, LANES), 1) < LANES // 2, high, square - high
     )
     qkv_send[...] = turned[...].reshape(B, 2 * G, D).astype(BF16)
-    qkv_recv[me] = qkv_send[my_request]
-
-    pl.semaphore_wait(barrier, len(ALL) + len(HEADS))
-
-    for offset in ALL:
-        copy_to(qkv_send.at[request_at(*offset)], qkv_recv.at[me], 0, peer(*offset))
+    pl.semaphore_wait(barrier, jnp.where(me < OWNERS, OWNERS - 1, OWNERS) + len(HEADS))
+
+    def send_qkv(step):
+        owner = lax.rem(me + step, OWNERS)
+        copy_to(qkv_send.at[owner], qkv_recv.at[me], 0, {"kvp": owner})
+
+    for step in range(1, OWNERS):
+        send_qkv(step)
+
+    @pl.when(me >= OWNERS)
+    def _():
+        send_qkv(0)
+
     for copy in copies[3:6]:
         copy.wait()
     sine, cosine = sine_and_cosine(lengths[my_request].astype(F32) * inverse[...])
@@ -239,20 +249,28 @@
     cosine = cosine[0:1]
     for copy in copies[6:10]:
         copy.wait()
-    waiter(qkv_recv.at[pl.ds(0, len(ALL))], 0).wait_recv()
-    total = jnp.sum(qkv_recv[...].astype(F32), axis=0)
-    square = total[SQUARE_ROW : SQUARE_ROW + 1]
-    square = square[:, 0:1] + square[:, LANES // 2 : LANES // 2 + 1]
-    total = total * lax.rsqrt(square / MODEL_WIDTH + EPSILON)
-    rotated = total * cosine + pltpu.roll(total, D // 2, 1) * sine
-    q_all[my_request] = rotated[:G].astype(BF16)
-    for offset in NEAR:
-        copy_to(q_all.at[my_request], q_all.at[my_request], 1, peer(*offset))
+
+    @pl.when(me < OWNERS)
+    def _():
+        qkv_recv[me] = qkv_send[my_request]
+        waiter(qkv_recv.at[pl.ds(0, N - 1)], 0).wait_recv()
+        total = jnp.sum(qkv_recv[...].astype(F32), axis=0)
+        square = total[SQUARE_ROW : SQUARE_ROW + 1]
+        square = square[:, 0:1] + square[:, LANES // 2 : LANES // 2 + 1]
+        total = total * lax.rsqrt(square / MODEL_WIDTH + EPSILON)
+        rotated = total * cosine + pltpu.roll(total, D // 2, 1) * sine
+        q_all[my_request] = rotated[:G].astype(BF16)
+        for offset in ALL:
+            copy_to(q_all.at[my_request], q_all.at[my_request], 1, peer(*offset))
+        pair[...] = jnp.where(iota((G, LANES), 0) == 0, rotated[G:], total[G:]).astype(BF16)
+        copy_to(pair, pair, 9, peer(Z // 2, 0))
+        waiter(q_all.at[pl.ds(0, OWNERS - 1)], 1).wait_recv()
+
+    @pl.when(me >= OWNERS)
+    def _():
+        waiter(q_all, 1).wait_recv()
+
     factor = D ** (-0.5)
-    new_key, new_value = rounded(rotated[G : G + 1]), rounded(total[G + 1 : G + 2])
-    own = jnp.sum(rounded(rotated[:G]) * new_key, axis=1, keepdims=True) * factor
-    waiter(q_all.at[pl.ds(0, len(NEAR))], 1).wait_recv()
-
     first = me * (PAGES_HERE * PAGE)
     slots = [[table[p, b] for p in range(PAGES_HERE)] for b in range(B)]
     scores = [
@@ -291,6 +309,13 @@
         copy_to(part_send.at[request_at(*offset)], part_recv.at[me], 2, peer(*offset))
     part_recv[me] = part_send[my_request]
     copies[10].wait()
+
+    @pl.when(me >= OWNERS)
+    def _():
+        waiter(pair, 9).wait_recv()
+
+    new_key, new_value = pair[...].astype(F32)[0:1], pair[...].astype(F32)[1:2]
+    own = jnp.sum(q_all[my_request].astype(F32) * new_key, axis=1, keepdims=True) * factor
     waiter(part_recv.at[pl.ds(0, len(ALL))], 2).wait_recv()
     tops, overall = [], own
     for k in range(N):
@@ -331,26 +356,38 @@
     square_row = to_row(jnp.sum(stream * stream, axis=1, keepdims=True))
     square_send[...] = square_row
     normed = (stream * mlp_gain[...][None, :].astype(F32)).astype(BF16)
-    for start in range(0, N, GROUP):
-        group = (ALL + [(0, 0)])[start : start + GROUP]
-        for offset in group:
-            tile = tile_at(*offset)
-            rows = pl.ds(pl.multiple_of(jnp.minimum(tile, tiles_ff - 1) * LANES, LANES), LANES)
-            for part in range(2):
-                ff_send[tile, part] = lax.dot_general(
-                    normed,
-                    win[part, rows, :],
-                    (((1,), (1,)), ((), ())),
-                    preferred_element_type=F32,
-                ).astype(BF16)
-        for offset in group:
-            if offset != (0, 0):
-                tile = tile_at(*offset)
-
-                @pl.when(tile < tiles_ff)
-                def _(tile=tile, offset=offset):
-                    copy_to(ff_send.at[tile], ff_recv.at[me], 5, peer(*offset))
-                    copy_to(square_send, square_recv.at[me], 6, peer(*offset))
+    tiles = [lax.rem(my_tile + step, tiles_ff) for step in range(tiles_ff)]
+    owners = [{"kvp": lax.rem(tile * SPREAD, N)} for tile in tiles]
+
+    def send_square(step):
+        copy_to(square_send, square_recv.at[me], 6, owners[step])
+
+    def make(step):
+        rows = pl.ds(pl.multiple_of(tiles[step] * LANES, LANES), LANES)
+        for part in range(2):
+            ff_send[tiles[step], part] = lax.dot_general(
+                normed,
+                win[part, rows, :],
+                (((1,), (1,)), ((), ())),
+                preferred_element_type=F32,
+            ).astype(BF16)
+
+    def send(step):
+        copy_to(ff_send.at[tiles[step]], ff_recv.at[me], 5, owners[step])
+
+    for step in range(1, tiles_ff):
+        send_square(step)
+    for start in range(1, tiles_ff, GROUP):
+        for step in range(start, min(start + GROUP, tiles_ff)):
+            make(step)
+        for step in range(start, min(start + GROUP, tiles_ff)):
+            send(step)
+    make(0)
+
+    @pl.when(my_tile >= tiles_ff)
+    def _():
+        send_square(0)
+        send(0)
 
     @pl.when(my_tile < tiles_ff)
     def _():
@@ -376,8 +413,16 @@
     term = jnp.dot(active, wdown[...], preferred_element_type=F32)
     out_ref[...] = (stream + over_heads(term, last_send, last_recv, 8)).astype(BF16)
 
-    waiter(qkv_recv.at[pl.ds(0, len(ALL))], 0).wait_send()
-    waiter(q_all.at[pl.ds(0, len(NEAR))], 1).wait_send()
+    @pl.when(me < OWNERS)
+    def _():
+        waiter(qkv_recv.at[pl.ds(0, OWNERS - 1)], 0).wait_send()
+        waiter(qkv_recv.at[pl.ds(0, N - 1), pl.ds(0, G)], 1).wait_send()
+        waiter(pair, 9).wait_send()
+
+    @pl.when(me >= OWNERS)
+    def _():
+        waiter(qkv_recv.at[pl.ds(0, OWNERS)], 0).wait_send()
+
     waiter(part_recv.at[pl.ds(0, len(ALL))], 2).wait_send()
     waiter(attn_all.at[pl.ds(0, len(NEAR))], 3).wait_send()
     waiter(head_recv.at[pl.ds(0, len(HEADS))], 4).wait_send()
@@ -417,7 +462,7 @@
     slots = k_cache.shape[1]
     return pl.pallas_call(
         functools.partial(kernel, tiles_ff, ff),
-        out_shape=jax.ShapeDtypeStruct((B, width), BF16),
+        out_shape=pltpu.VMEM((B, width), BF16),
         in_specs=[pl.BlockSpec(memory_space=pl.ANY)] * 12,
         out_specs=pl.BlockSpec(memory_space=pltpu.VMEM),
         scratch_shapes=[
@@ -437,13 +482,14 @@
             pltpu.VMEM((B, 2 * G, D), BF16),
             pltpu.VMEM((N, 2 * G, D), BF16),
             pltpu.VMEM((B, G, D), BF16),
+            pltpu.VMEM((G, D), BF16),
             pltpu.VMEM((B, 2 * G, D), BF16),
             pltpu.VMEM((N, 2 * G, D), BF16),
             pltpu.VMEM((B, G, D), BF16),
             pltpu.VMEM((B * G, D), F32),
             pltpu.VMEM((B, width), BF16),
             pltpu.VMEM((H, B, width), BF16),
-            pltpu.VMEM((N, 2, B, LANES), BF16),
+            pltpu.VMEM((tiles_ff, 2, B, LANES), BF16),
             pltpu.VMEM((N, 2, B, LANES), BF16),
             pltpu.VMEM((1, LANES), F32),
             pltpu.VMEM((N, 1, LANES), F32),
@@ -451,8 +497,8 @@
             pltpu.VMEM((B, width), BF16),
             pltpu.VMEM((H, B, width), BF16),
             pltpu.SemaphoreType.DMA((15,)),
-            pltpu.SemaphoreType.DMA((9,)),
-            pltpu.SemaphoreType.DMA((9,)),
+            pltpu.SemaphoreType.DMA((10,)),
+            pltpu.SemaphoreType.DMA((10,)),
         ],
         compiler_params=pltpu.CompilerParams(collective_id=0, has_side_effects=True),
     )(

time: 58.4 us -> 58 us (level)
  local copies, waits for them, and re-layouts: 1.3 us -> 0.6 us
    unnamed x1, local copies, waits for them, and re-layouts: 1.3 us -> 0.6 us
where the time goes in v3:
time: 58 us; the launch traced here: 57.8 us
  Pallas kernels  57.2 us (99%)
  local copies, waits for them, and re-layouts  0.6 us (1%)
    pallas_call x1, Pallas kernels, on_device(): pl.pallas_call(functools.partial(kernel, tiles_ff, ff), out_shape=pltpu.V...  57.2 us

profile of v3, /device:TPU:1, one launch (start us, length us, event | category | flops | bytes accessed | tf_op | source)
XLA Modules:
  0.0 57.8 jit_solution(13998354693801995227)
XLA Ops:
  0.0 57.2 %shard_map.118 = bf16[16,256]{1,0:T(8,128)(2,1)S(1)} custom-call(bf16[16,256]{1,0:T(8,128)(2,1)} %hidden_hbm.1, bf16[256]{0:T(256)(128)(2,1)} %attn_gain_hbm.1, bf16[256,1280]{1,0:T(8,128)(2,1)} %bitcast.9, bf16[64,128,128]{2,1,0:T(8,128)(2,1)} %bitcast.7, bf16[64,128,128]{2,1,0:T(8,128)(2,1)} %bitcast.8, s32[4,16]{1,0:T(4,128)} %bitcast.11, s32[16]{0:T(128)} %lengths_hbm.1, ...), custom_call_target="tpu_custom_call" | custom-call | tf_op jit(solution)/shard_map/pallas_call | solution.py:463
  57.2 0.6 %copy.14 = bf16[16,256]{1,0:T(8,128)(2,1)} copy(bf16[16,256]{1,0:T(8,128)(2,1)S(1)} %shard_map.118) | data formatting | bytes 16384

commit v4 on v3

--- a/solution.py
+++ b/solution.py
@@ -28,7 +28,7 @@
 VECTORS = G + 2
 LANES = 128
 SQUARE_ROW = VECTORS
-GROUP = 7
+GROUPS = (4, 6, 6, 5)
 OWNERS = 16
 SPREAD, UNSPREAD = 5, 13
 
@@ -129,6 +129,8 @@
     hid_all,
     last_send,
     last_recv,
+    owners,
+    tiles,
     local_sem,
     send_sem,
     recv_sem,
@@ -210,6 +212,19 @@
     for copy in copies[3:]:
         copy.start()
 
+    count, count_ff = 0, 0
+    for offset in ALL:
+        device = peer(*offset)["kvp"]
+        owners[count] = device
+        count = count + jnp.where(device < OWNERS, 1, 0)
+        tile = lax.rem(device * UNSPREAD, N)
+        tiles[count_ff] = tile
+        count_ff = count_ff + jnp.where(tile < tiles_ff, 1, 0)
+
+    @pl.when(my_tile < tiles_ff)
+    def _():
+        tiles[tiles_ff - 1] = my_tile
+
     pad = win.shape[1] - ff
     win[:, pl.ds(ff, pad), :] = jnp.zeros((2, pad, win.shape[2]), BF16)
     wdown[pl.ds(ff, pad), :] = jnp.zeros((pad, wdown.shape[1]), BF16)
@@ -231,15 +246,15 @@
     pl.semaphore_wait(barrier, jnp.where(me < OWNERS, OWNERS - 1, OWNERS) + len(HEADS))
 
     def send_qkv(step):
-        owner = lax.rem(me + step, OWNERS)
+        owner = owners[step]
         copy_to(qkv_send.at[owner], qkv_recv.at[me], 0, {"kvp": owner})
 
-    for step in range(1, OWNERS):
+    for step in range(OWNERS - 1):
         send_qkv(step)
 
     @pl.when(me >= OWNERS)
     def _():
-        send_qkv(0)
+        send_qkv(OWNERS - 1)
 
     for copy in copies[3:6]:
         copy.wait()
@@ -356,16 +371,18 @@
     square_row = to_row(jnp.sum(stream * stream, axis=1, keepdims=True))
     square_send[...] = square_row
     normed = (stream * mlp_gain[...][None, :].astype(F32)).astype(BF16)
-    tiles = [lax.rem(my_tile + step, tiles_ff) for step in range(tiles_ff)]
-    owners = [{"kvp": lax.rem(tile * SPREAD, N)} for tile in tiles]
+    ours = [tiles[step] for step in range(tiles_ff)]
+
+    def owner_of(step):
+        return {"kvp": lax.rem(ours[step] * SPREAD, N)}
 
     def send_square(step):
-        copy_to(square_send, square_recv.at[me], 6, owners[step])
+        copy_to(square_send, square_recv.at[me], 6, owner_of(step))
 
     def make(step):
-        rows = pl.ds(pl.multiple_of(tiles[step] * LANES, LANES), LANES)
+        rows = pl.ds(pl.multiple_of(ours[step] * LANES, LANES), LANES)
         for part in range(2):
-            ff_send[tiles[step], part] = lax.dot_general(
+            ff_send[ours[step], part] = lax.dot_general(
                 normed,
                 win[part, rows, :],
                 (((1,), (1,)), ((), ())),
@@ -373,21 +390,22 @@
             ).astype(BF16)
 
     def send(step):
-        copy_to(ff_send.at[tiles[step]], ff_recv.at[me], 5, owners[step])
-
-    for step in range(1, tiles_ff):
-        send_square(step)
-    for start in range(1, tiles_ff, GROUP):
-        for step in range(start, min(start + GROUP, tiles_ff)):
+        copy_to(ff_send.at[ours[step]], ff_recv.at[me], 5, owner_of(step))
+
+    start = 0
+    for size in GROUPS:
+        for step in range(start, start + size):
             make(step)
-        for step in range(start, min(start + GROUP, tiles_ff)):
+        for step in range(start, start + size):
             send(step)
-    make(0)
+            send_square(step)
+        start += size
+    make(start)
 
     @pl.when(my_tile >= tiles_ff)
     def _():
-        send_square(0)
-        send(0)
+        send(start)
+        send_square(start)
 
     @pl.when(my_tile < tiles_ff)
     def _():
@@ -496,6 +514,8 @@
             pltpu.VMEM((tiles_ff, B, LANES), BF16),
             pltpu.VMEM((B, width), BF16),
             pltpu.VMEM((H, B, width), BF16),
+            pltpu.SMEM((N,), jnp.int32),
+            pltpu.SMEM((N,), jnp.int32),
             pltpu.SemaphoreType.DMA((15,)),
             pltpu.SemaphoreType.DMA((10,)),
             pltpu.SemaphoreType.DMA((10,)),

time: 58 us -> 57.3 us (0.988)
  Pallas kernels: 57.2 us -> 56.6 us
    pallas_call x1, Pallas kernels: 57.2 us -> 56.6 us  [on_device(): pl.pallas_call(functools.partial(kernel, tiles_ff, ff), out_shape=pltpu.V...]
where the time goes in v4:
time: 57.3 us; the launch traced here: 57.2 us
  Pallas kernels  56.6 us (99%)
  local copies, waits for them, and re-layouts  0.6 us (1%)
    pallas_call x1, Pallas kernels, on_device(): pl.pallas_call(functools.partial(kernel, tiles_ff, ff), out_shape=pltpu.V...  56.6 us

profile of v4, /device:TPU:1, one launch (start us, length us, event | category | flops | bytes accessed | tf_op | source)
XLA Modules:
  0.0 57.2 jit_solution(13882052438031491368)
XLA Ops:
  0.0 56.6 %shard_map.118 = bf16[16,256]{1,0:T(8,128)(2,1)S(1)} custom-call(bf16[16,256]{1,0:T(8,128)(2,1)} %hidden_hbm.1, bf16[256]{0:T(256)(128)(2,1)} %attn_gain_hbm.1, bf16[256,1280]{1,0:T(8,128)(2,1)} %bitcast.9, bf16[64,128,128]{2,1,0:T(8,128)(2,1)} %bitcast.7, bf16[64,128,128]{2,1,0:T(8,128)(2,1)} %bitcast.8, s32[4,16]{1,0:T(4,128)} %bitcast.11, s32[16]{0:T(128)} %lengths_hbm.1, ...), custom_call_target="tpu_custom_call" | custom-call | tf_op jit(solution)/shard_map/pallas_call | solution.py:481
  56.6 0.6 %copy.14 = bf16[16,256]{1,0:T(8,128)(2,1)} copy(bf16[16,256]{1,0:T(8,128)(2,1)S(1)} %shard_map.118) | data formatting | bytes 16384
